TPU v7x, 128 devices: a whole 4x4x4 slice. The times are simulated.
128 devices in a mesh: shard: 32 (over z, y, x_lo), model: 4 (over x_hi, core).
Axes of the slice: x: 4 (x_hi: 2, x_lo: 2; x = x_hi * 2 + x_lo), y: 4, z: 4, core: 2. Of those that a mesh axis runs over, the one named last changes fastest.
Arguments:
- w_query: bfloat16 [12288, 12288], P('shard', 'model'), may hold values from -0.109375 to 0.109375
- low_query: bfloat16 [12288, 16], P('shard'), may hold values from -0.0546875 to 0.0546875
- high_query: bfloat16 [16, 12288], P(None, 'model'), may hold values from -1.5 to 1.5
- w_key: bfloat16 [12288, 12288], P('shard', 'model'), may hold values from -0.109375 to 0.109375
- low_key: bfloat16 [12288, 16], P('shard'), may hold values from -0.0546875 to 0.0546875
- high_key: bfloat16 [16, 12288], P(None, 'model'), may hold values from -1.5 to 1.5
- w_value: bfloat16 [12288, 12288], P('shard', 'model'), may hold values from -0.109375 to 0.109375
- low_value: bfloat16 [12288, 16], P('shard'), may hold values from -0.0546875 to 0.0546875
- high_value: bfloat16 [16, 12288], P(None, 'model'), may hold values from -1.5 to 1.5
- norm_gain: float32 [12288], P('shard'), may hold values from 0.25 to 1.75
Outputs:
- final_query: bfloat16 [12288, 12288], P(None, ('model', 'shard'))
- final_key: bfloat16 [12288, 12288], P(None, ('model', 'shard'))
- final_value: bfloat16 [12288, 12288], P(None, ('model', 'shard'))
- scale_query: float32 [12288], P(('model', 'shard'))
- scale_key: float32 [12288], P(('model', 'shard'))
- scale_value: float32 [12288], P(('model', 'shard'))
All inputs are finite; a program needn't handle non-finite values. Where the computation divides by a largest or mean magnitude, that divisor is 1e-20 or more.
Results may differ from a plain program's by a relative error of at most 0.001.
Values may be sent and summed in bfloat16 or wider, within the bound.
A program may use at most 128 MiB of HBM per device.

v0:
```python
import jax
import jax.numpy as jnp
from jax import lax
from jax.sharding import PartitionSpec as P

mix_rate = 1.0


def sent_to_all(value, axis):
    copies = jnp.broadcast_to(value, (lax.axis_size(axis), *value.shape))
    return lax.all_to_all(copies, axis, split_axis=0, concat_axis=0, tiled=True)


def over_copies(value, axis):
    everything = sent_to_all(value, axis)
    return jnp.max(everything, axis=0)


def together(arrays, axis):
    line, at, done = (jnp.concatenate([a.reshape(-1) for a in arrays]), 0, [])
    so_far = over_copies(line, axis)
    for a in arrays:
        done.append(so_far[at : at + a.size].reshape(a.shape))
        at += a.size
    return tuple(done)


def on_device(
    w_query,
    low_query,
    high_query,
    w_key,
    low_key,
    high_key,
    w_value,
    low_value,
    high_value,
    norm_gain,
):
    result_query = w_query.astype(jnp.float32) + mix_rate * jnp.dot(
        low_query, high_query, preferred_element_type=jnp.float32
    )
    result_key = w_key.astype(jnp.float32) + mix_rate * jnp.dot(
        low_key, high_key, preferred_element_type=jnp.float32
    )
    result_value = w_value.astype(jnp.float32) + mix_rate * jnp.dot(
        low_value, high_value, preferred_element_type=jnp.float32
    )
    result_gained_query = result_query * norm_gain[:, None]
    result_gained_key = result_key * norm_gain[:, None]
    result_gained_value = result_value * norm_gain[:, None]
    scale_query, scale_key, scale_value = together(
        (
            jnp.max(jnp.abs(result_gained_query), axis=0),
            jnp.max(jnp.abs(result_gained_key), axis=0),
            jnp.max(jnp.abs(result_gained_value), axis=0),
        ),
        "shard",
    )
    narrow_query, narrow_key, narrow_value = (
        (result_gained_query / scale_query).astype(jnp.bfloat16),
        (result_gained_key / scale_key).astype(jnp.bfloat16),
        (result_gained_value / scale_value).astype(jnp.bfloat16),
    )
    final_query, final_key, final_value = (
        lax.all_to_all(narrow_query, "shard", split_axis=1, concat_axis=0, tiled=True),
        lax.all_to_all(narrow_key, "shard", split_axis=1, concat_axis=0, tiled=True),
        lax.all_to_all(narrow_value, "shard", split_axis=1, concat_axis=0, tiled=True),
    )
    place = lax.axis_index("shard")
    scale_query = lax.dynamic_slice_in_dim(
        scale_query, place * final_query.shape[1], final_query.shape[1]
    )
    scale_key = lax.dynamic_slice_in_dim(scale_key, place * final_key.shape[1], final_key.shape[1])
    scale_value = lax.dynamic_slice_in_dim(
        scale_value, place * final_value.shape[1], final_value.shape[1]
    )
    return (final_query, final_key, final_value, scale_query, scale_key, scale_value)


def solution(mesh):
    return jax.shard_map(
        on_device,
        mesh=mesh,
        in_specs=(
            P("shard", "model"),
            P("shard", None),
            P(None, "model"),
            P("shard", "model"),
            P("shard", None),
            P(None, "model"),
            P("shard", "model"),
            P("shard", None),
            P(None, "model"),
            P("shard"),
        ),
        out_specs=(
            P(None, ("model", "shard")),
            P(None, ("model", "shard")),
            P(None, ("model", "shard")),
            P(("model", "shard")),
            P(("model", "shard")),
            P(("model", "shard")),
        ),
        check_vma=False,
    )
```

profile of v0, /device:TPU:0, one launch (start us, length us, event | category | flops | bytes accessed | tf_op | source)
XLA Modules:
  0.0 155.9 jit_solution(16265798905348577380)
XLA Ops:
  0.6 0.0 copy-start
  0.6 0.0 copy-start.5
  0.7 0.0 copy-start.6
  0.7 0.0 copy-start.3
  0.7 0.0 copy-start.1
  0.7 0.8 copy-done
  1.5 4.6 %abs_reduce_fusion.2 = (f32[3072]{0:T(1024)S(1)}, f32[384,3072]{1,0:T(8,128)}) fusion(f32[384]{0:T(512)} %param.19, bf16[384,16]{0,1:T(8,128)(2,1)} %param.11, bf16[16,3072]{1,0:T(8,128)(2,1)S(1)} %copy-done, bf16[384,3072]{1,0:T(8,128)(2,1)} %param.10), kind=kOutput, calls=%fused_computation.7 | convolution fusion | flops 43643904 | bytes 7202304 | tf_op jit(solution)/shard_map/dot_general | solution.py:40
  6.2 0.0 copy-done.5
  6.2 0.0 copy-done.6
  6.2 0.0 copy-done.3
  6.2 0.0 copy-done.1
  6.2 0.0 copy-start.2
  6.2 0.0 copy-start.4
  6.2 0.0 copy-start.7
  6.2 3.0 %abs_reduce_fusion = (f32[3072]{0:T(1024)S(1)}, f32[384,3072]{1,0:T(8,128)}) fusion(f32[384]{0:T(512)S(1)} %copy-done.5, bf16[384,16]{0,1:T(8,128)(2,1)S(1)} %copy-done.6, bf16[16,3072]{1,0:T(8,128)(2,1)S(1)} %copy-done.3, bf16[384,3072]{1,0:T(8,128)(2,1)S(1)} %copy-done.1), kind=kOutput, calls=%fused_computation.3 | convolution fusion | flops 43643904 | bytes 7202304 | tf_op jit(solution)/shard_map/dot_general | solution.py:46
  9.2 0.0 copy-done.2
  9.2 0.0 copy-done.4
  9.2 0.0 copy-done.7
  9.2 3.1 %abs_reduce_fusion.1 = (f32[3072]{0:T(1024)S(1)}, f32[384,3072]{1,0:T(8,128)}) fusion(f32[384]{0:T(512)S(1)} %copy-done.5, bf16[384,16]{0,1:T(8,128)(2,1)S(1)} %copy-done.7, bf16[16,3072]{1,0:T(8,128)(2,1)S(1)} %copy-done.4, bf16[384,3072]{1,0:T(8,128)(2,1)S(1)} %copy-done.2), kind=kOutput, calls=%fused_computation.5 | convolution fusion | flops 43643904 | bytes 7202304 | tf_op jit(solution)/shard_map/dot_general | solution.py:43
  12.3 0.6 broadcast_in_dim.2
  12.9 28.5 %all_to_all.63 = f32[32,1,9216]{2,1,0:T(1,128)S(1)} all-to-all(f32[32,1,9216]{2,1,0:T(1,128)S(1)} %broadcast_in_dim.2), channel_id=1, replica_groups=mesh['shard'=32,'model'=4] {'shard'}, dimensions={0} | all-to-all | bytes 2359296 | tf_op jit(solution)/shard_map/all_to_all | solution.py:11
  41.4 0.7 reduce_max.39
  42.0 2.8 %divide_convert_fusion.2 = bf16[384,3072]{1,0:T(8,128)(2,1)S(1)} fusion(f32[384,3072]{1,0:T(8,128)} %get-tuple-element.14, f32[3072]{0:T(1024)S(1)} %get-tuple-element.8), kind=kLoop, calls=%fused_computation.2 | loop fusion | flops 2359296 | bytes 7090176 | tf_op jit(solution)/shard_map/convert_element_type | solution.py:61
  44.9 2.4 %copy.35 = bf16[384,3072]{0,1:T(8,128)(2,1)} copy(bf16[384,3072]{1,0:T(8,128)(2,1)S(1)} %divide_convert_fusion.2) | data formatting | bytes 4718592 | tf_op jit(solution)/shard_map/convert_element_type | solution.py:61
  47.3 4.1 %all-to-all-start.1 = ((bf16[384,32,96]{0,2,1:T(8,128)(2,1)}), bf16[384,32,96]{0,2,1:T(8,128)(2,1)S(1)}, u32[]{:S(2)}, u32[]{:S(2)}) async-start(bf16[384,32,96]{0,2,1:T(8,128)(2,1)} %bitcast.20), calls=%async_computation.1 | async-start | bytes 4718592 | tf_op jit(solution)/shard_map/all_to_all | solution.py:66
  51.4 7.2 %divide_convert_fusion = (bf16[384,3072]{1,0:T(8,128)(2,1)}, bf16[384,3072]{1,0:T(8,128)(2,1)}) fusion(f32[384,3072]{1,0:T(8,128)} %get-tuple-element.10, f32[3072]{0:T(1024)S(1)} %get-tuple-element.6, f32[384,3072]{1,0:T(8,128)} %get-tuple-element.12, f32[3072]{0:T(1024)S(1)} %get-tuple-element.7), kind=kLoop, calls=%fused_computation | loop fusion | flops 4718592 | bytes 14180352 | tf_op jit(solution)/shard_map/convert_element_type | solution.py:63
  58.6 4.3 %copy.37 = bf16[384,3072]{0,1:T(8,128)(2,1)} copy(bf16[384,3072]{1,0:T(8,128)(2,1)} %get-tuple-element.16) | data formatting | bytes 4718592 | tf_op jit(solution)/shard_map/convert_element_type | solution.py:62
  62.9 20.1 %all-to-all-done.1 = bf16[384,32,96]{0,2,1:T(8,128)(2,1)S(1)} async-done(((bf16[384,32,96]{0,2,1:T(8,128)(2,1)}), bf16[384,32,96]{0,2,1:T(8,128)(2,1)S(1)}, u32[]{:S(2)}, u32[]{:S(2)}) %all-to-all-start.1) | async-done | bytes 2359328 | tf_op jit(solution)/shard_map/all_to_all | solution.py:66
  83.0 4.8 %all-to-all-start.2 = ((bf16[384,32,96]{0,2,1:T(8,128)(2,1)}), bf16[384,32,96]{0,2,1:T(8,128)(2,1)}, u32[]{:S(2)}, u32[]{:S(2)}) async-start(bf16[384,32,96]{0,2,1:T(8,128)(2,1)} %bitcast.21), calls=%async_computation.2 | async-start | bytes 4718592 | tf_op jit(solution)/shard_map/all_to_all | solution.py:67
  87.8 4.3 %copy.39 = bf16[384,3072]{0,1:T(8,128)(2,1)} copy(bf16[384,3072]{1,0:T(8,128)(2,1)} %get-tuple-element.15) | data formatting | bytes 4718592 | tf_op jit(solution)/shard_map/convert_element_type | solution.py:63
  92.0 25.5 %all-to-all-done.2 = bf16[384,32,96]{0,2,1:T(8,128)(2,1)} async-done(((bf16[384,32,96]{0,2,1:T(8,128)(2,1)}), bf16[384,32,96]{0,2,1:T(8,128)(2,1)}, u32[]{:S(2)}, u32[]{:S(2)}) %all-to-all-start.2) | async-done | bytes 2359328 | tf_op jit(solution)/shard_map/all_to_all | solution.py:67
  117.5 4.8 %all-to-all-start.3 = ((bf16[384,32,96]{0,2,1:T(8,128)(2,1)}), bf16[384,32,96]{0,2,1:T(8,128)(2,1)}, u32[]{:S(2)}, u32[]{:S(2)}) async-start(bf16[384,32,96]{0,2,1:T(8,128)(2,1)} %bitcast.19), calls=%async_computation.3 | async-start | bytes 4718592 | tf_op jit(solution)/shard_map/all_to_all | solution.py:68
  122.3 0.6 dynamic_slice.9
  122.9 0.6 dynamic_slice.10
  123.5 0.6 dynamic_slice.11
  124.1 1.7 %copy.45 = bf16[32,12,8,384]{3,2,0,1:T(8,128)(2,1)} copy(bf16[32,12,8,384]{3,2,1,0:T(8,128)(2,1)S(1)} %bitcast.18) | data formatting | bytes 4718592 | tf_op jit(solution)/shard_map/all_to_all | solution.py:66
  125.8 3.4 %copy.46 = bf16[32,12,8,384]{3,2,0,1:T(8,128)(2,1)} copy(bf16[32,12,8,384]{3,2,1,0:T(8,128)(2,1)} %bitcast.8) | data formatting | bytes 4718592 | tf_op jit(solution)/shard_map/all_to_all | solution.py:67
  129.2 23.3 %all-to-all-done.3 = bf16[384,32,96]{0,2,1:T(8,128)(2,1)} async-done(((bf16[384,32,96]{0,2,1:T(8,128)(2,1)}), bf16[384,32,96]{0,2,1:T(8,128)(2,1)}, u32[]{:S(2)}, u32[]{:S(2)}) %all-to-all-start.3) | async-done | bytes 2359328 | tf_op jit(solution)/shard_map/all_to_all | solution.py:68
  152.5 3.4 %copy.47 = bf16[32,12,8,384]{3,2,0,1:T(8,128)(2,1)} copy(bf16[32,12,8,384]{3,2,1,0:T(8,128)(2,1)} %bitcast.10) | data formatting | bytes 4718592 | tf_op jit(solution)/shard_map/all_to_all | solution.py:68
  (2 shorter events, 0.0 us)
Async XLA Ops:
  0.6 0.9 copy-start
  0.6 5.5 %copy-start.5 = (f32[384]{0:T(512)S(1)}, f32[384]{0:T(512)}, u32[]{:S(2)}) copy-start(f32[384]{0:T(512)} %param.19) | copy-start | bytes 4612
  0.7 5.5 %copy-start.6 = (bf16[384,16]{0,1:T(8,128)(2,1)S(1)}, bf16[384,16]{0,1:T(8,128)(2,1)}, u32[]{:S(2)}) copy-start(bf16[384,16]{0,1:T(8,128)(2,1)} %param.17) | copy-start | bytes 36868
  0.7 5.5 %copy-start.3 = (bf16[16,3072]{1,0:T(8,128)(2,1)S(1)}, bf16[16,3072]{1,0:T(8,128)(2,1)}, u32[]{:S(2)}) copy-start(bf16[16,3072]{1,0:T(8,128)(2,1)} %param.18) | copy-start | bytes 294916
  0.7 5.5 %copy-start.1 = (bf16[384,3072]{1,0:T(8,128)(2,1)S(1)}, bf16[384,3072]{1,0:T(8,128)(2,1)}, u32[]{:S(2)}) copy-start(bf16[384,3072]{1,0:T(8,128)(2,1)} %param.16) | copy-start | bytes 7077892
  6.2 3.0 %copy-start.2 = (bf16[384,3072]{1,0:T(8,128)(2,1)S(1)}, bf16[384,3072]{1,0:T(8,128)(2,1)}, u32[]{:S(2)}) copy-start(bf16[384,3072]{1,0:T(8,128)(2,1)} %param.13) | copy-start | bytes 7077892
  6.2 3.0 %copy-start.4 = (bf16[16,3072]{1,0:T(8,128)(2,1)S(1)}, bf16[16,3072]{1,0:T(8,128)(2,1)}, u32[]{:S(2)}) copy-start(bf16[16,3072]{1,0:T(8,128)(2,1)} %param.15) | copy-start | bytes 294916
  6.2 3.0 %copy-start.7 = (bf16[384,16]{0,1:T(8,128)(2,1)S(1)}, bf16[384,16]{0,1:T(8,128)(2,1)}, u32[]{:S(2)}) copy-start(bf16[384,16]{0,1:T(8,128)(2,1)} %param.14) | copy-start | bytes 36868
  47.3 35.6 %all-to-all-start.1 = ((bf16[384,32,96]{0,2,1:T(8,128)(2,1)}), bf16[384,32,96]{0,2,1:T(8,128)(2,1)S(1)}, u32[]{:S(2)}, u32[]{:S(2)}) async-start(bf16[384,32,96]{0,2,1:T(8,128)(2,1)} %bitcast.20), calls=%async_computation.1 | async-start | bytes 4718592 | tf_op jit(solution)/shard_map/all_to_all | solution.py:66
  83.0 34.6 %all-to-all-start.2 = ((bf16[384,32,96]{0,2,1:T(8,128)(2,1)}), bf16[384,32,96]{0,2,1:T(8,128)(2,1)}, u32[]{:S(2)}, u32[]{:S(2)}) async-start(bf16[384,32,96]{0,2,1:T(8,128)(2,1)} %bitcast.21), calls=%async_computation.2 | async-start | bytes 4718592 | tf_op jit(solution)/shard_map/all_to_all | solution.py:67
  117.5 34.9 %all-to-all-start.3 = ((bf16[384,32,96]{0,2,1:T(8,128)(2,1)}), bf16[384,32,96]{0,2,1:T(8,128)(2,1)}, u32[]{:S(2)}, u32[]{:S(2)}) async-start(bf16[384,32,96]{0,2,1:T(8,128)(2,1)} %bitcast.19), calls=%async_computation.3 | async-start | bytes 4718592 | tf_op jit(solution)/shard_map/all_to_all | solution.py:68
where the time goes:
time: 157 us; the launch traced here: 156 us
  waiting for transfers between devices  68.8 us (44%)
  blocking collectives  28.5 us (18%)
  local copies, waits for them, and re-layouts  22.7 us (14%)
  starting transfers between devices  13.7 us (9%)
  matrix products  10.7 us (7%)
  other arithmetic  10.7 us (7%)
    all_to_all x1, blocking collectives, sent_to_all(): return lax.all_to_all(copies, axis, split_axis=0, concat_axis=0, tiled=True)  28.5 us
    all_to_all x1, waiting for transfers between devices, on_device(): lax.all_to_all(narrow_key, 'shard', split_axis=1, concat_axis=0, tiled=True)  25.5 us
    all_to_all x1, waiting for transfers between devices, on_device(): lax.all_to_all(narrow_value, 'shard', split_axis=1, concat_axis=0, tiled=...  23.3 us
    all_to_all x1, waiting for transfers between devices, on_device(): lax.all_to_all(narrow_query, 'shard', split_axis=1, concat_axis=0, tiled=...  20.1 us
    convert_element_type x1, other arithmetic, on_device(): (result_gained_value / scale_value).astype(jnp.bfloat16)  7.22 us
    all_to_all x1, starting transfers between devices, on_device(): lax.all_to_all(narrow_value, 'shard', split_axis=1, concat_axis=0, tiled=...  4.8 us
    all_to_all x1, starting transfers between devices, on_device(): lax.all_to_all(narrow_key, 'shard', split_axis=1, concat_axis=0, tiled=True)  4.79 us
    dot_general x1, matrix products, on_device(): jnp.dot(low_query, high_query, preferred_element_type=jnp.float32)  4.65 us
  transfers between devices with their start and end apart: 3, of which 3 were waited for; matrix products, arithmetic and copies ran while one was open for 15% of the time, Pallas kernels for 0%

commit v1 on v0

v1 whole, which is shorter than its diff:
```python
import functools

import jax
import jax.numpy as jnp
from jax import lax
from jax.experimental import pallas as pl
from jax.experimental.pallas import tpu as pltpu
from jax.sharding import PartitionSpec as P

MESH = pl.DeviceIdType.MESH

NZ, NY, NX = 4, 4, 2
N = NZ * NY * NX
PARTS = 2


def hops(offset):
    dz, dy, dx = offset
    return min(dz, NZ - dz) + min(dy, NY - dy) + dx


OFFSETS = sorted(
    [(dz, dy, dx) for dz in range(NZ) for dy in range(NY) for dx in range(NX)][1:],
    key=lambda o: -hops(o),
)
PLANE = [(dz, dy) for dz in range(NZ) for dy in range(NY)][1:]


def exchange(*refs):
    (wq, wk, wv, lq, lk, lv, hq, hk, hv, gain_ref) = refs[:10]
    (out, scale_out) = refs[10:12]
    (wbuf, wt, land, gbuf, low_all, gain_all, ht, hrow) = refs[12:20]
    (load_sem, send_sem, recv_sem, low_send, low_recv, gain_send, gain_recv, relay_send, relay_gain) = refs[20:]
    rows = wq.shape[0]
    cols = land.shape[1]
    step = cols // PARTS
    rank = lq.shape[0]
    me = lax.axis_index("shard")
    mine = lax.axis_index("model")
    core = lax.rem(mine, 2)
    z, y, x = me // (NY * NX), lax.rem(me // NX, NY), lax.rem(me, NX)

    def there(offset):
        dz, dy, dx = offset
        return lax.rem(z + dz, NZ) * (NY * NX) + lax.rem(y + dy, NY) * NX + lax.rem(x + dx, NX)

    loads = []
    for m, w in enumerate((wq, wk, wv)):
        load = pltpu.make_async_copy(w, wbuf.at[m], load_sem.at[m])
        load.start()
        loads.append(load)

    other_core = {"model": mine + 1 - 2 * core}
    across = {"shard": me + 1 - 2 * x, "model": lax.rem(mine + 2, 4)}
    barrier = pltpu.get_barrier_semaphore()
    for o in OFFSETS:
        pl.semaphore_signal(barrier, inc=1, device_id={"shard": there(o)}, device_id_type=MESH)
    pl.semaphore_signal(barrier, inc=1, device_id=other_core, device_id_type=MESH)
    pl.semaphore_signal(barrier, inc=1, device_id=across, device_id_type=MESH)

    at_me = pl.ds(pl.multiple_of(me * rows, rows), rows)
    group = 4 * cols
    for m, (l, h) in enumerate(((lq, hq), (lk, hk), (lv, hv))):
        low_all[m, :, at_me] = l[...]
        part = h[:, pl.ds(pl.multiple_of((me // 4) * group, group), group)]
        hrow[...] = part.astype(jnp.float32).T
        ht[m] = hrow[pl.ds(pl.multiple_of(lax.rem(me, 4) * cols, 8), cols), :].astype(jnp.bfloat16)
    gain_all[:, at_me] = gain_ref[...].reshape(1, rows)

    for m in range(3):
        loads[m].wait()

        def turn(g, _):
            at = pl.ds(pl.multiple_of(g * group, group), group)
            wt[m, at, :] = wbuf[m, :, at].T
            return 0

        lax.fori_loop(0, wbuf.shape[2] // group, turn, 0)
        land[m, :, at_me] = wt[m, pl.ds(pl.multiple_of(me * cols, 16), cols), :]

    pl.semaphore_wait(barrier, N + 1)

    def low_copy(owner, send, recv, target):
        at = pl.ds(pl.multiple_of(owner * rows, rows), rows)
        return pltpu.make_async_remote_copy(
            src_ref=low_all.at[:, :, at], dst_ref=low_all.at[:, :, at],
            send_sem=send, recv_sem=recv, device_id=target, device_id_type=MESH,
        )

    def gain_copy(owner, send, recv, target):
        at = pl.ds(pl.multiple_of(owner * rows, rows), rows)
        return pltpu.make_async_remote_copy(
            src_ref=gain_all.at[:, at], dst_ref=gain_all.at[:, at],
            send_sem=send, recv_sem=recv, device_id=target, device_id_type=MESH,
        )

    for i, (dz, dy) in enumerate(PLANE):
        @pl.when(core == (dz + dy) % 2)
        def _():
            target = {"shard": there((dz, dy, 0))}
            low_copy(me, low_send.at[i], low_recv.at[me], target).start()
            gain_copy(me, gain_send.at[i], gain_recv.at[me], target).start()
    low_copy(me, relay_send.at[0, 0], low_recv.at[me], across).start()
    gain_copy(me, relay_gain.at[0, 0], gain_recv.at[me], across).start()

    def block_copy(m, p, i, o):
        t = there(o)
        at = pl.ds(pl.multiple_of(me * rows, rows), rows)
        return pltpu.make_async_remote_copy(
            src_ref=wt.at[m, pl.ds(pl.multiple_of(t * cols + p * step, 16), step), :],
            dst_ref=land.at[m, pl.ds(pl.multiple_of(p * step, 16), step), at],
            send_sem=send_sem.at[m * PARTS + p, i],
            recv_sem=recv_sem.at[m * PARTS + p, me],
            device_id={"shard": t}, device_id_type=MESH,
        )

    def send_slot(slot, _):
        m, p = slot // PARTS, lax.rem(slot, PARTS)
        for i, o in enumerate(OFFSETS):
            block_copy(m, p, i, o).start()
        return 0

    lax.fori_loop(0, 3 * PARTS, send_slot, 0)

    for i, (dz, dy) in enumerate(PLANE):
        @pl.when(core == (dz + dy) % 2)
        def _():
            owner = there((NZ - dz, NY - dy, 0))
            low_copy(owner, low_send.at[i], low_recv.at[owner], other_core).wait_recv()
            gain_copy(owner, gain_send.at[i], gain_recv.at[owner], other_core).wait_recv()
            for k, target in ((1, other_core), (2, across)):
                low_copy(owner, relay_send.at[k, i + 1], low_recv.at[owner], target).start()
                gain_copy(owner, relay_gain.at[k, i + 1], gain_recv.at[owner], target).start()
    flip = 1 - 2 * x
    for i, (dz, dy) in enumerate(PLANE):
        @pl.when(core == (dz + dy) % 2)
        def _():
            owner = there((NZ - dz, NY - dy, 0)) + flip
            low_copy(owner, low_send.at[i], low_recv.at[owner], other_core).wait_recv()
            gain_copy(owner, gain_send.at[i], gain_recv.at[owner], other_core).wait_recv()
            low_copy(owner, relay_send.at[3, i + 1], low_recv.at[owner], other_core).start()
            gain_copy(owner, relay_gain.at[3, i + 1], gain_recv.at[owner], other_core).start()
    low_copy(me + flip, relay_send.at[0, 0], low_recv.at[me + flip], other_core).wait_recv()
    gain_copy(me + flip, relay_gain.at[0, 0], gain_recv.at[me + flip], other_core).wait_recv()
    for i, (dz, dy) in enumerate(PLANE):
        @pl.when(core != (dz + dy) % 2)
        def _():
            for owner in (there((NZ - dz, NY - dy, 0)), there((NZ - dz, NY - dy, 0)) + flip):
                low_copy(owner, low_send.at[i], low_recv.at[owner], other_core).wait_recv()
                gain_copy(owner, gain_send.at[i], gain_recv.at[owner], other_core).wait_recv()

    for m in range(3):
        for p in range(PARTS):
            lines = slice(p * step, (p + 1) * step)
            slot = m * PARTS + p

            def gained(source):
                at = pl.ds(pl.multiple_of(source * rows, rows), rows)
                update = jnp.dot(ht[m, lines, :], low_all[m, :, at], preferred_element_type=jnp.float32)
                r = (land[m, lines, at].astype(jnp.float32) + update) * gain_all[:, at]
                gbuf[lines, at] = r
                a = jnp.abs(r)
                return jnp.maximum(jnp.maximum(a[:, 0:128], a[:, 128:256]), a[:, 256:384])

            top = gained(me)

            def collect(i, top):
                source = lax.rem(me + 1 + i, N)
                at = pl.ds(pl.multiple_of(source * rows, rows), rows)
                pltpu.make_async_remote_copy(
                    src_ref=wt.at[m, pl.ds(0, step), :],
                    dst_ref=land.at[m, pl.ds(p * step, step), at],
                    send_sem=send_sem.at[slot, 0], recv_sem=recv_sem.at[slot, source],
                    device_id=other_core, device_id_type=MESH,
                ).wait_recv()
                return jnp.maximum(top, gained(source))

            top = lax.fori_loop(0, N - 1, collect, top)
            scale = jnp.max(top, axis=1, keepdims=True)
            scale_out[m, lines, :] = jnp.broadcast_to(scale, (step, 128))
            inverse = 1.0 / scale

            def finish(source, _):
                at = pl.ds(pl.multiple_of(source * rows, rows), rows)
                out[m, lines, at] = (gbuf[lines, at] * inverse).astype(out.dtype)
                return 0

            lax.fori_loop(0, N, finish, 0)

    def sent_slot(slot, _):
        m, p = slot // PARTS, lax.rem(slot, PARTS)
        for i, o in enumerate(OFFSETS):
            block_copy(m, p, i, o).wait_send()
        return 0

    lax.fori_loop(0, 3 * PARTS, sent_slot, 0)
    low_copy(me, relay_send.at[0, 0], low_recv.at[me], across).wait_send()
    gain_copy(me, relay_gain.at[0, 0], gain_recv.at[me], across).wait_send()
    for i, (dz, dy) in enumerate(PLANE):
        @pl.when(core == (dz + dy) % 2)
        def _():
            low_copy(me, low_send.at[i], low_recv.at[me], other_core).wait_send()
            gain_copy(me, gain_send.at[i], gain_recv.at[me], other_core).wait_send()
            for k in (1, 2, 3):
                low_copy(me, relay_send.at[k, i + 1], low_recv.at[me], other_core).wait_send()
                gain_copy(me, relay_gain.at[k, i + 1], gain_recv.at[me], other_core).wait_send()


def deliver(out, scale, fq, fk, fv, sq, sk, sv, row, sem):
    copies = []
    for m, f in enumerate((fq, fk, fv)):
        copy = pltpu.make_async_copy(out.at[m], f, sem.at[m])
        copy.start()
        copies.append(copy)
    for m, s in enumerate((sq, sk, sv)):
        s[...] = scale[m].T[0:1, :]
    for copy in copies:
        copy.wait()


def on_device(wq, lq, hq, wk, lk, hk, wv, lv, hv, gain):
    rows, width = wq.shape
    rank = lq.shape[1]
    cols = width // N
    total = rows * N
    f32, bf16 = jnp.float32, jnp.bfloat16
    vmem = pl.BlockSpec(memory_space=pltpu.VMEM)
    anywhere = pl.BlockSpec(memory_space=pl.ANY)
    dma = pltpu.SemaphoreType.DMA
    out, scale = pl.pallas_call(
        exchange,
        out_shape=(
            pltpu.VMEM((3, cols, total), bf16),
            pltpu.VMEM((3, cols, 128), f32),
        ),
        in_specs=[anywhere] * 3 + [vmem] * 7,
        out_specs=(vmem, vmem),
        scratch_shapes=[
            pltpu.VMEM((3, rows, width), bf16),
            pltpu.VMEM((3, width, rows), bf16),
            pltpu.VMEM((3, cols, total), bf16),
            pltpu.VMEM((cols, total), f32),
            pltpu.VMEM((3, rank, total), bf16),
            pltpu.VMEM((1, total), f32),
            pltpu.VMEM((3, cols, rank), bf16),
            pltpu.VMEM((4 * cols, rank), f32),
            dma((3,)),
            dma((3 * PARTS, N)),
            dma((3 * PARTS, N)),
            dma((16,)),
            dma((N,)),
            dma((16,)),
            dma((N,)),
            dma((4, 16)),
            dma((4, 16)),
        ],
        compiler_params=pltpu.CompilerParams(
            collective_id=0, has_side_effects=True, vmem_limit_bytes=52 * 2**20
        ),
    )(wq, wk, wv, lq.T, lk.T, lv.T, hq, hk, hv, gain)
    final = jax.ShapeDtypeStruct((cols, total), bf16)
    line = jax.ShapeDtypeStruct((1, cols), f32)
    fq, fk, fv, sq, sk, sv = pl.pallas_call(
        deliver,
        out_shape=(final, final, final, line, line, line),
        in_specs=[vmem, vmem],
        out_specs=(anywhere,) * 3 + (vmem,) * 3,
        scratch_shapes=[pltpu.VMEM((8, 128), f32), dma((3,))],
        compiler_params=pltpu.CompilerParams(vmem_limit_bytes=2 * 2**20),
    )(
        pltpu.with_memory_space_constraint(out, pltpu.VMEM),
        pltpu.with_memory_space_constraint(scale, pltpu.VMEM),
    )
    return fq.T, fk.T, fv.T, sq.reshape(cols), sk.reshape(cols), sv.reshape(cols)


def solution(mesh):
    weight, low, high = P("shard", "model"), P("shard", None), P(None, "model")
    final, scale = P(None, ("model", "shard")), P(("model", "shard"))
    return jax.shard_map(
        on_device,
        mesh=mesh,
        in_specs=(weight, low, high) * 3 + (P("shard"),),
        out_specs=(final,) * 3 + (scale,) * 3,
        check_vma=False,
    )
```

time: 157 us -> 106 us (0.68)
  Pallas kernels: 0 us -> 104 us
  waiting for transfers between devices: 68.8 us -> 0 us
  blocking collectives: 28.5 us -> 0 us
  local copies, waits for them, and re-layouts: 22.7 us -> 0 us
  starting transfers between devices: 13.7 us -> 0 us
  matrix products: 10.7 us -> 0 us
  other arithmetic: 10.7 us -> 0 us
    pallas_call x0 -> x2, Pallas kernels: none -> 104 us  [the longest x1 101 us: on_device(): pl.pallas_call(exchange, out_shape=(pltpu.VMEM((3, cols, total), bf16), p...]
    all_to_all x3 -> x0, waiting for transfers between devices: 68.8 us -> none  [the longest x1 25.5 us: on_device(): lax.all_to_all(narrow_key, 'shard', split_axis=1, concat_axis=0, tiled=True)]
    all_to_all x1 -> x0, blocking collectives: 28.5 us -> none  [sent_to_all(): return lax.all_to_all(copies, axis, split_axis=0, concat_axis=0, tiled=True)]
    all_to_all x3 -> x0, starting transfers between devices: 13.7 us -> none  [the longest x1 4.8 us: on_device(): lax.all_to_all(narrow_value, 'shard', split_axis=1, concat_axis=0, tiled=...]
    convert_element_type x3 -> x0, local copies, waits for them, and re-layouts: 11 us -> none  [the longest x1 4.28 us: on_device(): (result_gained_key / scale_key).astype(jnp.bfloat16)]
    dot_general x3 -> x0, matrix products: 10.7 us -> none  [the longest x1 4.65 us: on_device(): jnp.dot(low_query, high_query, preferred_element_type=jnp.float32)]
    convert_element_type x2 -> x0, other arithmetic: 10 us -> none  [the longest x1 7.22 us: on_device(): (result_gained_value / scale_value).astype(jnp.bfloat16)]
    all_to_all x3 -> x0, local copies, waits for them, and re-layouts: 8.5 us -> none  [the longest x1 3.39 us: on_device(): lax.all_to_all(narrow_value, 'shard', split_axis=1, concat_axis=0, tiled=...]
  transfers between devices with their start and end apart: 3 -> 0, of which waited for: 3 -> 0; matrix products, arithmetic and copies ran while one was open for 15% -> 0% of each run, Pallas kernels for 0% -> 0%
where the time goes in v1:
time: 106 us; the launch traced here: 105 us
  Pallas kernels  104 us (98%)
    pallas_call x1, Pallas kernels, on_device(): pl.pallas_call(exchange, out_shape=(pltpu.VMEM((3, cols, total), bf16), p...  101 us
    pallas_call x1, Pallas kernels, on_device(): pl.pallas_call(deliver, out_shape=(final, final, final, line, line, line)...  3.5 us

profile of v1, /device:TPU:0, one launch (start us, length us, event | category | flops | bytes accessed | tf_op | source)
XLA Modules:
  0.0 105.1 jit_solution(16537406375152750903)
XLA Ops:
  0.6 100.9 %shard_map.145 = (bf16[3,96,12288]{2,1,0:T(8,128)(2,1)S(1)}, f32[3,96,128]{2,1,0:T(8,128)S(1)}) custom-call(bf16[384,3072]{1,0:T(8,128)(2,1)} %refs_0_.1, bf16[384,3072]{1,0:T(8,128)(2,1)} %refs_1_.1, bf16[384,3072]{1,0:T(8,128)(2,1)} %refs_2_.1, bf16[16,384]{1,0:T(8,128)(2,1)} %bitcast.9, bf16[16,384]{1,0:T(8,128)(2,1)} %bitcast.10, ...), custom_call_target="tpu_custom_call" | custom-call | tf_op jit(solution)/shard_map/pallas_call | solution.py:230
  101.5 3.5 %shard_map.146 = (bf16[96,12288]{1,0:T(8,128)(2,1)}, bf16[96,12288]{1,0:T(8,128)(2,1)}, bf16[96,12288]{1,0:T(8,128)(2,1)}, f32[1,96]{1,0:T(1,128)}, f32[1,96]{1,0:T(1,128)}, /*index=5*/f32[1,96]{1,0:T(1,128)}) custom-call(bf16[3,96,12288]{2,1,0:T(8,128)(2,1)S(1)} %get-tuple-element.14.out, f32[3,96,128]{2,1,0:T(8,128)S(1)} %get-tuple-element.15.scale), custom_call_target="tpu_custom_call" | custom-call | tf_op jit(solution)/shard_map/pallas_call | solution.py:263

commit v2 on v1

v2 whole, which is shorter than its diff:
```python
import jax
import jax.numpy as jnp
from jax import lax
from jax.experimental import pallas as pl
from jax.experimental.pallas import tpu as pltpu
from jax.sharding import PartitionSpec as P

MESH = pl.DeviceIdType.MESH

NZ, NY, NX = 4, 4, 2
N = NZ * NY * NX
CUTS = (((0, 3), (3, 3)), ((0, 3), (3, 3)), ((0, 3), (3, 3)))
SLOTS = [(m, a, n) for m, cuts in enumerate(CUTS) for a, n in cuts]
CHUNKS = 8


def hops(offset):
    dz, dy, dx = offset
    return min(dz, NZ - dz) + min(dy, NY - dy) + dx


OFFSETS = sorted(
    [(dz, dy, dx) for dz in range(NZ) for dy in range(NY) for dx in range(NX)][1:],
    key=lambda o: -hops(o),
)
PLANE = [(dz, dy) for dz in range(NZ) for dy in range(NY)][1:]


def exchange(*refs):
    weights, lows, highs, gain_ref = refs[0:3], refs[3:6], refs[6:9], refs[9]
    out, scale_out = refs[10:12]
    (wbuf, wt, land, gbuf, low_all, gain_all, ht, hrow, hbuf, gbuf_in) = refs[12:22]
    (load_sem, small_sem, send_sem, recv_sem, low_send, low_recv, gain_send, gain_recv) = refs[22:]
    rows = wbuf.shape[1]
    cols = land.shape[1]
    unit = cols // 6
    group = 4 * cols
    groups = wbuf.shape[2] // group
    me = lax.axis_index("shard")
    mine = lax.axis_index("model")
    core = lax.rem(mine, 2)
    z, y, x = me // (NY * NX), lax.rem(me // NX, NY), lax.rem(me, NX)

    def there(offset):
        dz, dy, dx = offset
        return lax.rem(z + dz, NZ) * (NY * NX) + lax.rem(y + dy, NY) * NX + lax.rem(x + dx, NX)

    def span(owner):
        return pl.ds(pl.multiple_of(owner * rows, rows), rows)

    def load(m, g):
        at = pl.ds(g * group, group)
        return pltpu.make_async_copy(weights[m].at[:, at], wbuf.at[m, :, at], load_sem.at[m, g])

    for g in range(groups):
        load(0, g).start()
    small = [pltpu.make_async_copy(lows[m], low_all.at[m, :, span(me)], small_sem.at[m]) for m in range(3)]
    small.append(pltpu.make_async_copy(gain_ref, gbuf_in, small_sem.at[3]))
    highs_in = [pltpu.make_async_copy(highs[m], hbuf.at[m], small_sem.at[4 + m]) for m in range(3)]
    for copy in small + highs_in:
        copy.start()

    other_core = {"model": mine + 1 - 2 * core}
    across = {"shard": me + 1 - 2 * x, "model": lax.rem(mine + 2, 4)}
    barrier = pltpu.get_barrier_semaphore()
    for o in OFFSETS:
        pl.semaphore_signal(barrier, inc=1, device_id={"shard": there(o)}, device_id_type=MESH)
    pl.semaphore_signal(barrier, inc=1, device_id=other_core, device_id_type=MESH)
    pl.semaphore_signal(barrier, inc=1, device_id=across, device_id_type=MESH)

    def turned(m):
        for g in range(groups):
            load(m, g).wait()
            at = slice(g * group, (g + 1) * group)
            wt[m, at, :] = wbuf[m, :, at].T

    def block_copy(slot, i, o):
        m, a, n = SLOTS[slot]
        t = there(o)
        return pltpu.make_async_remote_copy(
            src_ref=wt.at[m, pl.ds(pl.multiple_of(t * cols + a * unit, 16), n * unit), :],
            dst_ref=land.at[m, pl.ds(a * unit, n * unit), span(me)],
            send_sem=send_sem.at[slot, i], recv_sem=recv_sem.at[slot, me],
            device_id={"shard": t}, device_id_type=MESH,
        )

    def sent(m):
        for slot, (of, _, _) in enumerate(SLOTS):
            if of == m:
                for i, o in enumerate(OFFSETS):
                    block_copy(slot, i, o).start()
        land[m, :, span(me)] = wt[m, pl.ds(pl.multiple_of(me * cols, 16), cols), :]

    def pair(owner, slot, target):
        return (
            pltpu.make_async_remote_copy(
                src_ref=low_all.at[:, :, span(owner)], dst_ref=low_all.at[:, :, span(owner)],
                send_sem=low_send.at[slot], recv_sem=low_recv.at[owner],
                device_id=target, device_id_type=MESH,
            ),
            pltpu.make_async_remote_copy(
                src_ref=gain_all.at[:, span(owner)], dst_ref=gain_all.at[:, span(owner)],
                send_sem=gain_send.at[slot], recv_sem=gain_recv.at[owner],
                device_id=target, device_id_type=MESH,
            ),
        )

    def launch(owner, slot, target):
        for copy in pair(owner, slot, target):
            copy.start()

    def landed(owner):
        for copy in pair(owner, 0, other_core):
            copy.wait_recv()

    def left(slot):
        for copy in pair(me, slot, other_core):
            copy.wait_send()

    flip = 1 - 2 * x

    turned(0)
    for m in (1, 2):
        for g in range(groups):
            load(m, g).start()
    for copy in small:
        copy.wait()
    gain_all[:, span(me)] = gbuf_in[...].reshape(1, rows)
    pl.semaphore_wait(barrier, N + 1)

    for i, (dz, dy) in enumerate(PLANE):
        @pl.when(core == (dz + dy) % 2)
        def _():
            launch(me, i, {"shard": there((dz, dy, 0))})
    launch(me, 15, across)
    sent(0)
    turned(1)
    sent(1)
    turned(2)
    sent(2)

    for m in range(3):
        highs_in[m].wait()
        part = hbuf[m, :, pl.ds(pl.multiple_of((me // 4) * group, group), group)]
        hrow[...] = part.astype(jnp.float32).T
        ht[m] = hrow[pl.ds(pl.multiple_of(lax.rem(me, 4) * cols, 8), cols), :].astype(ht.dtype)

    for i, (dz, dy) in enumerate(PLANE):
        @pl.when(core == (dz + dy) % 2)
        def _():
            owner = there((NZ - dz, NY - dy, 0))
            landed(owner)
            launch(owner, 16 + i, other_core)
            launch(owner, 31 + i, across)
    for i, (dz, dy) in enumerate(PLANE):
        @pl.when(core == (dz + dy) % 2)
        def _():
            owner = there((NZ - dz, NY - dy, 0)) + flip
            landed(owner)
            launch(owner, 46 + i, other_core)
    landed(me + flip)
    for i, (dz, dy) in enumerate(PLANE):
        @pl.when(core != (dz + dy) % 2)
        def _():
            landed(there((NZ - dz, NY - dy, 0)))
            landed(there((NZ - dz, NY - dy, 0)) + flip)

    def long(c):
        width = gbuf.shape[1] // CHUNKS
        return pl.ds(pl.multiple_of(c * width, width), width)

    for slot, (m, a, n) in enumerate(SLOTS):
        lines = slice(a * unit, (a + n) * unit)
        count = n * unit

        def product(c, _):
            gbuf[lines, long(c)] = jnp.dot(
                ht[m, lines, :], low_all[m, :, long(c)], preferred_element_type=jnp.float32
            )
            return 0

        lax.fori_loop(0, CHUNKS, product, 0)

        def arrive(i, _):
            source = lax.rem(me + 1 + i, N)
            pltpu.make_async_remote_copy(
                src_ref=wt.at[m, pl.ds(0, count), :],
                dst_ref=land.at[m, pl.ds(a * unit, count), span(source)],
                send_sem=send_sem.at[slot, 0], recv_sem=recv_sem.at[slot, source],
                device_id=other_core, device_id_type=MESH,
            ).wait_recv()
            return 0

        lax.fori_loop(0, N - 1, arrive, 0)

        def gained(c, top):
            at = long(c)
            r = (land[m, lines, at].astype(jnp.float32) + gbuf[lines, at]) * gain_all[:, at]
            gbuf[lines, at] = r
            r = jnp.abs(r)
            for b in range(r.shape[1] // 128):
                top = jnp.maximum(top, r[:, b * 128 : (b + 1) * 128])
            return top

        top = lax.fori_loop(0, CHUNKS, gained, jnp.zeros((count, 128), jnp.float32))
        scale = jnp.max(top, axis=1, keepdims=True)
        scale_out[m, lines, :] = jnp.broadcast_to(scale, (count, 128))
        inverse = 1.0 / scale

        def finish(c, _):
            out[m, lines, long(c)] = (gbuf[lines, long(c)] * inverse).astype(out.dtype)
            return 0

        lax.fori_loop(0, CHUNKS, finish, 0)

    for slot in range(len(SLOTS)):
        for i, o in enumerate(OFFSETS):
            block_copy(slot, i, o).wait_send()

    left(15)
    for i, (dz, dy) in enumerate(PLANE):
        @pl.when(core == (dz + dy) % 2)
        def _():
            for slot in (i, 16 + i, 31 + i, 46 + i):
                left(slot)


def deliver(out, scale, fq, fk, fv, sq, sk, sv, sem):
    half = out.shape[1] // 2
    copies = []
    for m, f in enumerate((fq, fk, fv)):
        for b in range(2):
            at = pl.ds(b * half, half)
            copy = pltpu.make_async_copy(out.at[m, at], f.at[at], sem.at[m, b])
            copy.start()
            copies.append(copy)
    for m, s in enumerate((sq, sk, sv)):
        s[...] = scale[m].T[0:1, :]
    for copy in copies:
        copy.wait()


def on_device(wq, lq, hq, wk, lk, hk, wv, lv, hv, gain):
    rows, width = wq.shape
    rank = lq.shape[1]
    cols = width // N
    total = rows * N
    slots = len(SLOTS)
    f32, bf16 = jnp.float32, jnp.bfloat16
    vmem = pl.BlockSpec(memory_space=pltpu.VMEM)
    anywhere = pl.BlockSpec(memory_space=pl.ANY)
    dma = pltpu.SemaphoreType.DMA
    out, scale = pl.pallas_call(
        exchange,
        out_shape=(
            pltpu.VMEM((3, cols, total), bf16),
            pltpu.VMEM((3, cols, 128), f32),
        ),
        in_specs=[anywhere] * 10,
        out_specs=(vmem, vmem),
        scratch_shapes=[
            pltpu.VMEM((3, rows, width), bf16),
            pltpu.VMEM((3, width, rows), bf16),
            pltpu.VMEM((3, cols, total), bf16),
            pltpu.VMEM((cols, total), f32),
            pltpu.VMEM((3, rank, total), bf16),
            pltpu.VMEM((1, total), f32),
            pltpu.VMEM((3, cols, rank), bf16),
            pltpu.VMEM((4 * cols, rank), f32),
            pltpu.VMEM((3, rank, width), bf16),
            pltpu.VMEM((rows,), f32),
            dma((3, 8)),
            dma((7,)),
            dma((slots, N)),
            dma((slots, N)),
            dma((61,)),
            dma((N,)),
            dma((61,)),
            dma((N,)),
        ],
        compiler_params=pltpu.CompilerParams(
            collective_id=0, has_side_effects=True, vmem_limit_bytes=52 * 2**20
        ),
    )(wq, wk, wv, lq.T, lk.T, lv.T, hq, hk, hv, gain)
    final = jax.ShapeDtypeStruct((cols, total), bf16)
    line = jax.ShapeDtypeStruct((1, cols), f32)
    fq, fk, fv, sq, sk, sv = pl.pallas_call(
        deliver,
        out_shape=(final, final, final, line, line, line),
        in_specs=[vmem, vmem],
        out_specs=(anywhere,) * 3 + (vmem,) * 3,
        scratch_shapes=[dma((3, 2))],
        compiler_params=pltpu.CompilerParams(vmem_limit_bytes=2 * 2**20),
    )(
        pltpu.with_memory_space_constraint(out, pltpu.VMEM),
        pltpu.with_memory_space_constraint(scale, pltpu.VMEM),
    )
    return fq.T, fk.T, fv.T, sq.reshape(cols), sk.reshape(cols), sv.reshape(cols)


def solution(mesh):
    weight, low, high = P("shard", "model"), P("shard", None), P(None, "model")
    final, scale = P(None, ("model", "shard")), P(("model", "shard"))
    return jax.shard_map(
        on_device,
        mesh=mesh,
        in_specs=(weight, low, high) * 3 + (P("shard"),),
        out_specs=(final,) * 3 + (scale,) * 3,
        check_vma=False,
    )
```

time: 106 us -> 99.9 us (0.942)
  Pallas kernels: 104 us -> 98.7 us
    pallas_call x1, Pallas kernels: 101 us -> 95.2 us  [on_device(): pl.pallas_call(exchange, out_shape=(pltpu.VMEM((3, cols, total), bf16), p...]
where the time goes in v2:
time: 99.9 us; the launch traced here: 99.3 us
  Pallas kernels  98.7 us (99%)
    pallas_call x1, Pallas kernels, on_device(): pl.pallas_call(exchange, out_shape=(pltpu.VMEM((3, cols, total), bf16), p...  95.2 us
    pallas_call x1, Pallas kernels, on_device(): pl.pallas_call(deliver, out_shape=(final, final, final, line, line, line)...  3.49 us

profile of v2, /device:TPU:0, one launch (start us, length us, event | category | flops | bytes accessed | tf_op | source)
XLA Modules:
  0.0 99.3 jit_solution(1104688802130190985)
XLA Ops:
  0.6 95.2 %shard_map.145 = (bf16[3,96,12288]{2,1,0:T(8,128)(2,1)S(1)}, f32[3,96,128]{2,1,0:T(8,128)S(1)}) custom-call(bf16[384,3072]{1,0:T(8,128)(2,1)} %refs_0_.1, bf16[384,3072]{1,0:T(8,128)(2,1)} %refs_1_.1, bf16[384,3072]{1,0:T(8,128)(2,1)} %refs_2_.1, bf16[16,384]{1,0:T(8,128)(2,1)} %bitcast.9, bf16[16,384]{1,0:T(8,128)(2,1)} %bitcast.10, ...), custom_call_target="tpu_custom_call" | custom-call | tf_op jit(solution)/shard_map/pallas_call | solution.py:253
  95.8 3.5 %shard_map.146 = (bf16[96,12288]{1,0:T(8,128)(2,1)}, bf16[96,12288]{1,0:T(8,128)(2,1)}, bf16[96,12288]{1,0:T(8,128)(2,1)}, f32[1,96]{1,0:T(1,128)}, f32[1,96]{1,0:T(1,128)}, /*index=5*/f32[1,96]{1,0:T(1,128)}) custom-call(bf16[3,96,12288]{2,1,0:T(8,128)(2,1)S(1)} %get-tuple-element.14.out, f32[3,96,128]{2,1,0:T(8,128)S(1)} %get-tuple-element.15.scale), custom_call_target="tpu_custom_call" | custom-call | tf_op jit(solution)/shard_map/pallas_call | solution.py:287

commit v3 on v2

--- a/solution.py
+++ b/solution.py
@@ -23,6 +23,8 @@
     [(dz, dy, dx) for dz in range(NZ) for dy in range(NY) for dx in range(NX)][1:],
     key=lambda o: -hops(o),
 )
+NEXT = [(0, 0, 1)]
+REST = [o for o in OFFSETS if o not in NEXT]
 PLANE = [(dz, dy) for dz in range(NZ) for dy in range(NY)][1:]
 
 
@@ -84,12 +86,18 @@
             device_id={"shard": t}, device_id_type=MESH,
         )
 
+    def start(slots, chosen):
+        for slot in slots:
+            for i, o in enumerate(OFFSETS):
+                if o in chosen:
+                    block_copy(slot, i, o).start()
+
+    def own(m):
+        land[m, :, span(me)] = wt[m, pl.ds(pl.multiple_of(me * cols, 16), cols), :]
+
     def sent(m):
-        for slot, (of, _, _) in enumerate(SLOTS):
-            if of == m:
-                for i, o in enumerate(OFFSETS):
-                    block_copy(slot, i, o).start()
-        land[m, :, span(me)] = wt[m, pl.ds(pl.multiple_of(me * cols, 16), cols), :]
+        start([slot for slot, (of, _, _) in enumerate(SLOTS) if of == m], REST)
+        own(m)
 
     def pair(owner, slot, target):
         return (
@@ -128,6 +136,7 @@
     gain_all[:, span(me)] = gbuf_in[...].reshape(1, rows)
     pl.semaphore_wait(barrier, N + 1)
 
+    start(range(2), NEXT)
     for i, (dz, dy) in enumerate(PLANE):
         @pl.when(core == (dz + dy) % 2)
         def _():
@@ -135,8 +144,10 @@
     launch(me, 15, across)
     sent(0)
     turned(1)
+    start((2, 3), NEXT)
     sent(1)
     turned(2)
+    start((4, 5), NEXT)
     sent(2)
 
     for m in range(3):
@@ -181,20 +192,19 @@
 
         lax.fori_loop(0, CHUNKS, product, 0)
 
-        def arrive(i, _):
-            source = lax.rem(me + 1 + i, N)
+        def waited(source):
             pltpu.make_async_remote_copy(
                 src_ref=wt.at[m, pl.ds(0, count), :],
                 dst_ref=land.at[m, pl.ds(a * unit, count), span(source)],
                 send_sem=send_sem.at[slot, 0], recv_sem=recv_sem.at[slot, source],
                 device_id=other_core, device_id_type=MESH,
             ).wait_recv()
+
+        def arrive(i, _):
+            waited(lax.rem(me + 1 + i, N))
             return 0
 
-        lax.fori_loop(0, N - 1, arrive, 0)
-
-        def gained(c, top):
-            at = long(c)
+        def gained(at, top):
             r = (land[m, lines, at].astype(jnp.float32) + gbuf[lines, at]) * gain_all[:, at]
             gbuf[lines, at] = r
             r = jnp.abs(r)
@@ -202,7 +212,16 @@
                 top = jnp.maximum(top, r[:, b * 128 : (b + 1) * 128])
             return top
 
-        top = lax.fori_loop(0, CHUNKS, gained, jnp.zeros((count, 128), jnp.float32))
+        top = jnp.zeros((count, 128), jnp.float32)
+        if slot < len(SLOTS) - 1:
+            lax.fori_loop(0, N - 1, arrive, 0)
+            top = lax.fori_loop(0, CHUNKS, lambda c, top: gained(long(c), top), top)
+        else:
+            top = gained(span(me), top)
+            for dz, dy, dx in NEXT + REST:
+                source = there((NZ - dz, NY - dy, NX - dx))
+                waited(source)
+                top = gained(span(source), top)
         scale = jnp.max(top, axis=1, keepdims=True)
         scale_out[m, lines, :] = jnp.broadcast_to(scale, (count, 128))
         inverse = 1.0 / scale
@@ -225,17 +244,19 @@
                 left(slot)
 
 
-def deliver(out, scale, fq, fk, fv, sq, sk, sv, sem):
+def deliver(out, scale, fq, fk, fv, sq, sk, sv, line, sem, line_sem):
     half = out.shape[1] // 2
     copies = []
     for m, f in enumerate((fq, fk, fv)):
         for b in range(2):
             at = pl.ds(b * half, half)
-            copy = pltpu.make_async_copy(out.at[m, at], f.at[at], sem.at[m, b])
-            copy.start()
-            copies.append(copy)
+            copies.append(pltpu.make_async_copy(out.at[m, at], f.at[at], sem.at[m, b]))
+            copies[-1].start()
     for m, s in enumerate((sq, sk, sv)):
-        s[...] = scale[m].T[0:1, :]
+        line[m] = scale[m].T[0:1, :]
+        copies.append(pltpu.make_async_copy(line.at[m], s, line_sem.at[m]))
+    for copy in copies[6:]:
+        copy.start()
     for copy in copies:
         copy.wait()
 
@@ -288,8 +309,8 @@
         deliver,
         out_shape=(final, final, final, line, line, line),
         in_specs=[vmem, vmem],
-        out_specs=(anywhere,) * 3 + (vmem,) * 3,
-        scratch_shapes=[dma((3, 2))],
+        out_specs=(anywhere,) * 6,
+        scratch_shapes=[pltpu.VMEM((3, 1, cols), f32), dma((3, 2)), dma((3,))],
         compiler_params=pltpu.CompilerParams(vmem_limit_bytes=2 * 2**20),
     )(
         pltpu.with_memory_space_constraint(out, pltpu.VMEM),

time: 99.9 us -> 98.5 us (0.986)
  Pallas kernels: 98.7 us -> 97.7 us
where the time goes in v3:
time: 98.5 us; the launch traced here: 98.4 us
  Pallas kernels  97.7 us (99%)
    pallas_call x1, Pallas kernels, on_device(): pl.pallas_call(exchange, out_shape=(pltpu.VMEM((3, cols, total), bf16), p...  94.7 us
    pallas_call x1, Pallas kernels, on_device(): pl.pallas_call(deliver, out_shape=(final, final, final, line, line, line)...  3.01 us

profile of v3, /device:TPU:0, one launch (start us, length us, event | category | flops | bytes accessed | tf_op | source)
XLA Modules:
  0.0 98.4 jit_solution(9100831331953419130)
XLA Ops:
  0.6 94.7 %shard_map.145 = (bf16[3,96,12288]{2,1,0:T(8,128)(2,1)S(1)}, f32[3,96,128]{2,1,0:T(8,128)S(1)}) custom-call(bf16[384,3072]{1,0:T(8,128)(2,1)} %refs_0_.1, bf16[384,3072]{1,0:T(8,128)(2,1)} %refs_1_.1, bf16[384,3072]{1,0:T(8,128)(2,1)} %refs_2_.1, bf16[16,384]{1,0:T(8,128)(2,1)} %bitcast.9, bf16[16,384]{1,0:T(8,128)(2,1)} %bitcast.10, ...), custom_call_target="tpu_custom_call" | custom-call | tf_op jit(solution)/shard_map/pallas_call | solution.py:274
  95.3 3.0 %shard_map.146 = (bf16[96,12288]{1,0:T(8,128)(2,1)}, bf16[96,12288]{1,0:T(8,128)(2,1)}, bf16[96,12288]{1,0:T(8,128)(2,1)}, f32[1,96]{1,0:T(1,128)}, f32[1,96]{1,0:T(1,128)}, /*index=5*/f32[1,96]{1,0:T(1,128)}) custom-call(bf16[3,96,12288]{2,1,0:T(8,128)(2,1)S(1)} %get-tuple-element.14.out, f32[3,96,128]{2,1,0:T(8,128)S(1)} %get-tuple-element.15.scale), custom_call_target="tpu_custom_call" | custom-call | tf_op jit(solution)/shard_map/pallas_call | solution.py:308

commit v4 on v3

--- a/solution.py
+++ b/solution.py
@@ -180,6 +180,17 @@
         width = gbuf.shape[1] // CHUNKS
         return pl.ds(pl.multiple_of(c * width, width), width)
 
+    def settled():
+        for slot in range(len(SLOTS) - 1):
+            for i, o in enumerate(OFFSETS):
+                block_copy(slot, i, o).wait_send()
+        left(15)
+        for i, (dz, dy) in enumerate(PLANE):
+            @pl.when(core == (dz + dy) % 2)
+            def _():
+                for slot in (i, 16 + i, 31 + i, 46 + i):
+                    left(slot)
+
     for slot, (m, a, n) in enumerate(SLOTS):
         lines = slice(a * unit, (a + n) * unit)
         count = n * unit
@@ -191,6 +202,9 @@
             return 0
 
         lax.fori_loop(0, CHUNKS, product, 0)
+
+        if slot == len(SLOTS) - 1:
+            settled()
 
         def waited(source):
             pltpu.make_async_remote_copy(
@@ -232,16 +246,8 @@
 
         lax.fori_loop(0, CHUNKS, finish, 0)
 
-    for slot in range(len(SLOTS)):
-        for i, o in enumerate(OFFSETS):
-            block_copy(slot, i, o).wait_send()
-
-    left(15)
-    for i, (dz, dy) in enumerate(PLANE):
-        @pl.when(core == (dz + dy) % 2)
-        def _():
-            for slot in (i, 16 + i, 31 + i, 46 + i):
-                left(slot)
+    for i, o in enumerate(OFFSETS):
+        block_copy(len(SLOTS) - 1, i, o).wait_send()
 
 
 def deliver(out, scale, fq, fk, fv, sq, sk, sv, line, sem, line_sem):

time: 98.5 us -> 98.3 us (level)
  no operation moved by 1% of the time
where the time goes in v4:
time: 98.3 us; the launch traced here: 98 us
  Pallas kernels  97.3 us (99%)
    pallas_call x1, Pallas kernels, on_device(): pl.pallas_call(exchange, out_shape=(pltpu.VMEM((3, cols, total), bf16), p...  94.3 us
    pallas_call x1, Pallas kernels, on_device(): pl.pallas_call(deliver, out_shape=(final, final, final, line, line, line)...  3.01 us

profile of v4, /device:TPU:0, one launch (start us, length us, event | category | flops | bytes accessed | tf_op | source)
XLA Modules:
  0.0 98.0 jit_solution(17356105576317713299)
XLA Ops:
  0.6 94.3 %shard_map.145 = (bf16[3,96,12288]{2,1,0:T(8,128)(2,1)S(1)}, f32[3,96,128]{2,1,0:T(8,128)S(1)}) custom-call(bf16[384,3072]{1,0:T(8,128)(2,1)} %refs_0_.1, bf16[384,3072]{1,0:T(8,128)(2,1)} %refs_1_.1, bf16[384,3072]{1,0:T(8,128)(2,1)} %refs_2_.1, bf16[16,384]{1,0:T(8,128)(2,1)} %bitcast.9, bf16[16,384]{1,0:T(8,128)(2,1)} %bitcast.10, ...), custom_call_target="tpu_custom_call" | custom-call | tf_op jit(solution)/shard_map/pallas_call | solution.py:280
  95.0 3.0 %shard_map.146 = (bf16[96,12288]{1,0:T(8,128)(2,1)}, bf16[96,12288]{1,0:T(8,128)(2,1)}, bf16[96,12288]{1,0:T(8,128)(2,1)}, f32[1,96]{1,0:T(1,128)}, f32[1,96]{1,0:T(1,128)}, /*index=5*/f32[1,96]{1,0:T(1,128)}) custom-call(bf16[3,96,12288]{2,1,0:T(8,128)(2,1)S(1)} %get-tuple-element.14.out, f32[3,96,128]{2,1,0:T(8,128)S(1)} %get-tuple-element.15.scale), custom_call_target="tpu_custom_call" | custom-call | tf_op jit(solution)/shard_map/pallas_call | solution.py:314
